TPU v7x, 32 devices: a 4x4x1 block of a 4x4x8 slice. The times are simulated.
32 devices in a mesh: data: 1 (over z), inner: 4 (over y), stage: 8 (over x, core).
Axes of the slice: x: 4, y: 4, z: 1, core: 2. Of those that a mesh axis runs over, the one named last changes fastest.
The devices are a block of a 4x4x8 slice.
Arguments:
- x: bfloat16 [8, 256, 1024], P(('data', 'stage'), 'inner')
- g: bfloat16 [8, 256, 1024], P(('data', 'stage'), 'inner')
- w1: bfloat16 [1, 8, 1024, 4096], P(None, 'stage')
- w2: bfloat16 [1, 8, 4096, 1024], P(None, 'stage')
Outputs:
- output 1: bfloat16 [8, 256, 1024], P(('data', 'stage'), 'inner')
- output 2: bfloat16 [8, 256, 1024], P(('data', 'stage'), 'inner')
- output 3: float32 [1, 8, 1024, 4096], P('data', 'stage')
- output 4: float32 [1, 8, 4096, 1024], P('data', 'stage')
All inputs are finite; a program needn't handle non-finite values.
Results may differ from a plain program's by a relative error of at most 0.02.
Values are sent between devices in bfloat16 or wider.
A program may use at most 768 MiB of HBM per device.

v0:
```python
import functools

import jax
import jax.numpy as jnp
from jax import lax
from jax.experimental import pallas as pl
from jax.experimental.pallas import tpu as pltpu
from jax.sharding import PartitionSpec as P

MESH = pl.DeviceIdType.MESH
F32, BF16 = jnp.float32, jnp.bfloat16
C0, C1 = 0.7978845608028654, 0.044715
LANES = 128
VMEM_LIMIT = 67043328
SLABS = 4
MERGE = 2
EARLY = 2
DEEP = 3
PRE_LATE = 2


def _gelu_and_slope(z):
    z2 = z * z
    half = 0.5 * jnp.tanh(z * (C0 + (C0 * C1) * z2)) + 0.5
    a = z * half
    return a, half + (a - a * half) * (2.0 * C0 + (6.0 * C0 * C1) * z2)


def _dot(a, b):
    return jnp.dot(a, b, preferred_element_type=F32)


def _wide(slabs):
    return jnp.concatenate(slabs, axis=1)


def _tall(parts):
    return jnp.concatenate(parts, axis=0)


def _cut(value, c):
    return value[:, c * LANES : (c + 1) * LANES]


def _rows_of(read, ks, n):
    return _tall([_wide([read(k, c) for c in range(n)]) for k in ks])


def _chunks(rows, groups, group_rows):
    step = max(1, rows // group_rows)
    for k in range(0, groups, step):
        ks = range(k, min(k + step, groups))
        yield ks, slice(k * group_rows, (k + len(ks)) * group_rows)


def _dw_block(
    rows, hg, gg, groups, group_rows, nd, w1_block, w2t_block, ht, ab, zb, put, ready=None
):
    for ks, s in _chunks(rows, groups, group_rows):
        if ready is None:
            z = _dot(_rows_of(hg, ks, nd), w1_block())
        da = _dot(_rows_of(gg, ks, nd), w2t_block())
        if ready is None:
            a, slope = _gelu_and_slope(z)
            a = a.astype(BF16)
            for c in range(SLABS):
                ab[c, s, :] = _cut(a, c)
        else:
            slope = _rows_of(ready[1], ks, SLABS)
        dz = (da * slope).astype(BF16)
        for c in range(SLABS):
            zb[c, s, :] = _cut(dz, c)
    a = _wide([ab[c] for c in range(SLABS)] if ready is None else [ready[0](c) for c in range(SLABS)])
    v2 = lax.dot_general(
        a, _rows_of(gg, range(groups), nd), (((0,), (0,)), ((), ())), preferred_element_type=F32
    )
    put(_dot(_wide([ht[t] for t in range(ht.shape[0])]), _wide([zb[c] for c in range(SLABS)])), v2)


def _transposed_rows(hg, groups, group_rows, nd, ht):
    per = LANES // group_rows
    for t in range(groups // per):
        ht[t] = _tall([_wide([hg(t * per + e, c) for c in range(nd)]) for e in range(per)]).T


def _chain_kernel(
    n_stage, n_inner, x, g, w1, w2, y, dx, h_late, g_late, w1_out, w2_out, d1_part, d2_part, a_pre, s_pre,
    w1v, w2v, w1t, w2t, hw, gw, ho, go, zs, act, ht, narrow, full, own_v,
    wsem, xsem, h_recv, g_recv, h_send, g_send, out_recv, ring_send, ring_recv, part_sem, late_sem, pre_sem, keep_sem, own_sem,
):
    p, i = lax.axis_index("stage"), lax.axis_index("inner")
    right, left = lax.rem(i + 1, n_inner), lax.rem(i + n_inner - 1, n_inner)
    _, m_all, nd, rows, _ = hw.shape
    nf = w1v.shape[0]
    units = nf // SLABS
    early = EARLY
    last = n_stage - 1
    half = nd // 2
    part = rows // MERGE
    mid = n_stage // 2
    groups = n_inner * early
    tokens = groups * rows
    ab, zb = narrow.at[0], narrow.at[1]

    def flat(ref, c):
        return ref.at[0, :, c * LANES : (c + 1) * LANES]

    mine = [
        pltpu.make_async_copy(flat(src, c), own_v.at[n, c], own_sem.at[n]) for n, src in enumerate((x, g)) for c in range(nd)
    ]
    for c in mine:
        c.start()

    barrier = pltpu.get_barrier_semaphore()
    for q in range(1, n_stage):
        pl.semaphore_signal(barrier, inc=1, device_id={"stage": lax.rem(p + q, n_stage)}, device_id_type=MESH)
    for q in (left, right):
        pl.semaphore_signal(barrier, inc=1, device_id={"inner": q}, device_id_type=MESH)

    loads = [
        pltpu.make_async_copy(w1.at[0, 0, :, c * LANES : (c + 1) * LANES], w1v.at[c], wsem.at[0]) for c in range(nf)
    ] + [pltpu.make_async_copy(w2.at[0, 0, :, c * LANES : (c + 1) * LANES], w2v.at[c], wsem.at[1]) for c in range(nd)]
    for c in loads:
        c.start()

    def to_stage(src, dst, send, recv, stage):
        return pltpu.make_async_remote_copy(
            src_ref=src, dst_ref=dst, send_sem=send, recv_sem=recv,
            device_id={"stage": stage}, device_id_type=MESH,
        )

    def to_inner(src, dst, send, recv, inner):
        return pltpu.make_async_remote_copy(
            src_ref=src, dst_ref=dst, send_sem=send, recv_sem=recv,
            device_id={"inner": inner}, device_id_type=MESH,
        )

    def piece(e):
        return pl.ds(pl.multiple_of(e * part, part), part)

    with jax.named_scope("barrier"):
        pl.semaphore_wait(barrier, n_stage + 1)
    for c in mine:
        c.wait()

    def own(mine_v, slots, recv, sem, stage):
        there = slots.at[i, p // MERGE, :, piece(p % MERGE)]

        @pl.when(p == stage)
        def _():
            pltpu.make_async_copy(mine_v, there, recv.at[p // MERGE]).start()

        @pl.when(p != stage)
        def _():
            to_stage(mine_v, there, sem, recv.at[p // MERGE], stage).start()

    own(own_v.at[0], hw, h_recv, xsem.at[0], 0)
    own(own_v.at[1], gw, g_recv, xsem.at[1], last)

    def ring_first(q, m, whole):
        a = whole.at[i, m]
        to_inner(a, a, ring_send.at[q, m, 0], ring_recv.at[q, m, 0], right).start()
        to_inner(a, a, ring_send.at[q, m, 1], ring_recv.at[q, m, 1], left).start()

    def ring_forward(q, m, whole):
        a, b = whole.at[left, m], whole.at[right, m]
        to_inner(a, a, ring_send.at[q, m, 0], ring_recv.at[q, m, 0], right).wait_recv()
        a = whole.at[left, m, pl.ds(0, half)]
        to_inner(a, a, ring_send.at[q, m, 2], ring_recv.at[q, m, 2], right).start()
        to_inner(b, b, ring_send.at[q, m, 1], ring_recv.at[q, m, 1], left).wait_recv()
        b = whole.at[right, m, pl.ds(half, half)]
        to_inner(b, b, ring_send.at[q, m, 3], ring_recv.at[q, m, 3], left).start()

    def ring_far(q, m, whole):
        far = lax.rem(i + 2, n_inner)
        a, b = whole.at[far, m, pl.ds(0, half)], whole.at[far, m, pl.ds(half, half)]
        return (
            to_inner(a, a, ring_send.at[q, m, 2], ring_recv.at[q, m, 2], right),
            to_inner(b, b, ring_send.at[q, m, 3], ring_recv.at[q, m, 3], left),
        )

    def ring_arrived(m, q):
        for c in ring_far(q, m, (hw, gw)[q]):
            c.wait_recv()

    def ring_sent(m):
        for q, whole in ((0, hw), (1, gw)):
            for c in ring_far(q, m, whole):
                c.wait_send()
            a = whole.at[i, m]
            to_inner(a, a, ring_send.at[q, m, 0], ring_recv.at[q, m, 0], right).wait_send()
            to_inner(a, a, ring_send.at[q, m, 1], ring_recv.at[q, m, 1], left).wait_send()

    def pass_on(m, lo, hi, src, slots, send, recv, end, nxt, out, out_sem):
        @pl.when(p != end)
        def _():
            some = pl.ds(lo, hi - lo)
            to_stage(src.at[m, some], slots.at[i, m, some], send.at[m], recv.at[m], nxt).start()

        if hi - lo < nd:
            return

        @pl.when(p == end)
        def _():
            for e in range(MERGE):
                home = m * MERGE + e

                @pl.when(p != home)
                def _():
                    for c in range(nd):
                        to_stage(src.at[m, c, piece(e)], flat(out, c), send.at[m], out_sem, home).start()

                @pl.when(p == home)
                def _():
                    for c in range(nd):
                        pltpu.make_async_copy(src.at[m, c, piece(e)], flat(out, c), out_sem).start()

    def project(m, split, res, w, src, *rest):
        whole = _wide([act[c] for c in range(nf)])
        count = half if split else nd
        for lo in range(0, nd, count):
            u = _dot(whole, _wide([w[lo + c] for c in range(count)]))
            out = (res[:, lo * LANES : (lo + count) * LANES].astype(F32) + u).astype(BF16)
            for c in range(count):
                src[m, lo + c] = _cut(out, c)
            pass_on(m, lo, lo + count, src, *rest)

    def forward(m, sloped, split):
        with jax.named_scope("wait_h"):
            pltpu.make_async_copy(hw.at[i, m], hw.at[i, m], h_recv.at[m]).wait()
        h = _wide([hw[i, m, c] for c in range(nd)])
        for b in range(0, nf, SLABS):
            z = _dot(h, _wide([w1v[b + c] for c in range(SLABS)]))
            a, slope = _gelu_and_slope(z)
            a, kept = a.astype(BF16), slope if sloped else z
            for c in range(SLABS):
                zs[m, b + c] = _cut(kept, c)
                act[b + c] = _cut(a, c)

        @pl.when((m == 0) & (p < n_stage // 2))
        def _():
            for c in loads[nf:]:
                c.wait()

        project(m, split, h, w2v, ho, hw, h_send, h_recv, last, jnp.minimum(p + 1, last), y, out_recv.at[0])

        @pl.when((p < mid) | (m < early))
        def _():
            ring_first(0, m, hw)

    def backward(m, split):
        @pl.when((p >= mid) & (p < n_stage - 2) & (m == early + 1))
        def _():
            ring_forward(1, early - 1, gw)

        with jax.named_scope("wait_g"):
            pltpu.make_async_copy(gw.at[i, m], gw.at[i, m], g_recv.at[m]).wait()

        @pl.when(m < early)
        def _():
            ring_first(1, m, gw)

        dh = _wide([gw[i, m, c] for c in range(nd)])
        for b in range(0, nf, SLABS):
            da = _dot(dh, _wide([w2t[b + c] for c in range(SLABS)]))
            dz = (da * _wide([zs[m, b + c] for c in range(SLABS)])).astype(BF16)
            for c in range(SLABS):
                act[b + c] = _cut(dz, c)
        project(m, split, dh, w1t, go, gw, g_send, g_recv, 0, jnp.maximum(p - 1, 0), dx, out_recv.at[1])

        @pl.when((p >= n_stage - 2) & (m == early))
        def _():
            ring_forward(0, 0, hw)

        @pl.when((p < mid) & (m > 0) & (m <= early))
        def _():
            ring_forward(1, jnp.maximum(m - 1, 0), gw)

        @pl.when((p >= mid) & (p < n_stage - 2) & (m == early))
        def _():
            ring_forward(1, 0, gw)

    def transpose_weights():
        def some(c, carry):
            s = pl.ds(pl.multiple_of(c * LANES, LANES), LANES)
            for e in range(nd):
                w1t[e, s, :] = w1v[c, e * LANES : (e + 1) * LANES, :].T
                w2t[c, e * LANES : (e + 1) * LANES, :] = w2v[e, s, :].T
            return carry

        lax.fori_loop(0, nf, some, 0)

    def slopes():
        def some(t, carry):
            m, b = t // (nf // SLABS), t % (nf // SLABS) * SLABS
            for c in range(SLABS):
                zs[m, b + c] = _gelu_and_slope(zs[m, b + c])[1]
            return carry

        lax.fori_loop(0, m_all * (nf // SLABS), some, 0)

    def each(lo, hi, fn):
        lax.fori_loop(lo, hi, lambda m, c: (fn(m), c)[1], 0)

    def group(whole, part=0):
        return lambda k, c: whole[k // early, part * early + k % early, c]

    def pre_stores(j):
        b = j % 2
        return (
            pltpu.make_async_copy(narrow.at[b], a_pre.at[j], pre_sem.at[0, b]),
            pltpu.make_async_copy(full.at[b, pl.ds(0, SLABS * groups)], s_pre.at[j], pre_sem.at[1, b]),
        )

    def pre_loads(j):
        b = j % 2
        return (
            pltpu.make_async_copy(
                a_pre.at[j], w2v.at[pl.ds(b * SLABS, SLABS), pl.ds(0, tokens)], pre_sem.at[0, b]
            ),
            pltpu.make_async_copy(s_pre.at[j], zs.at[b, pl.ds(0, SLABS * groups)], pre_sem.at[1, b]),
        )

    def pre_unit(j):
        b = j % 2

        @pl.when(j > 1)
        def _():
            for c in pre_stores(j):
                c.wait()

        for ks, s in _chunks(256, groups, rows):
            z = _dot(_rows_of(group(hw, j // units), ks, nd), _wide([w1v[j % units * SLABS + c] for c in range(SLABS)]))
            a, slope = _gelu_and_slope(z)
            a = a.astype(BF16)
            for c in range(SLABS):
                narrow[b, c, s, :] = _cut(a, c)
                for n, k in enumerate(ks):
                    full[b, c * groups + k] = _cut(slope[n * rows : (n + 1) * rows], c)
        for c in pre_stores(j):
            c.start()

    formed = jnp.where(
        p < PRE_LATE, 2 * units, jnp.where(p < mid - 1, units, jnp.where(p == mid - 1, units // 2, 0))
    )

    def part_copies(j):
        b, some = j % 2, pl.ds(0, SLABS * nd)
        return (
            pltpu.make_async_copy(full.at[b, some], d1_part.at[j], part_sem.at[0, b]),
            pltpu.make_async_copy(zs.at[m_all - 2 + b, some], d2_part.at[j], part_sem.at[1, b]),
        )

    def late_copies():
        return [
            pltpu.make_async_copy(whole.at[k, pl.ds(early, m_all - early)], out.at[k], late_sem.at[q, k])
            for q, (whole, out) in enumerate(((hw, h_late), (gw, g_late)))
            for k in range(n_inner)
        ]

    def sent(m):
        ring_sent(m)
        for src, slots, send, recv, end in ((ho, hw, h_send, h_recv, last), (go, gw, g_send, g_recv, 0)):
            for e in range(MERGE):
                a = src.at[m, :, piece(e)]

                @pl.when((p != end) | (p != m * MERGE + e))
                def _():
                    to_stage(a, a, send.at[m], recv.at[m], 0).wait_send()

        @pl.when((m == 0) & (p != 0))
        def _():
            to_stage(own_v.at[0], own_v.at[0], xsem.at[0], h_recv.at[0], 0).wait_send()

        @pl.when((m == 0) & (p != last))
        def _():
            to_stage(own_v.at[1], own_v.at[1], xsem.at[1], g_recv.at[0], last).wait_send()

    def unit(j):
        def forwards(m):
            @pl.when(p >= mid)
            def _():
                ring_forward(0, m, hw)

            ring_forward(1, m, gw)

        def firsts(m):
            @pl.when(p >= mid)
            def _():
                ring_first(0, m, hw)

            ring_first(1, m, gw)

        @pl.when(j == 0)
        def _():
            @pl.when(p >= n_stage - 2)
            def _():
                ring_forward(1, 0, gw)
                each(1, early, lambda e: (ring_forward(0, e, hw), ring_forward(1, e, gw)))


            @pl.when(p < n_stage // 2)
            def _():
                for c in pre_loads(0):
                    c.start()

            each(0, early, lambda m: ring_arrived(m, 1))

            @pl.when(p >= n_stage // 2)
            def _():
                each(0, early, lambda m: ring_arrived(m, 0))

            each(early, m_all, firsts)

            @pl.when(p >= mid)
            def _():
                _transposed_rows(group(hw), groups, rows, nd, ht)

        for m in range(early, m_all):
            @pl.when(j == 2 * (m - early + 1) + jnp.where(p < mid, 0, 1))
            def _():
                forwards(m)

        @pl.when(j == units - 1)
        def _():
            each(early, m_all, lambda m: ring_arrived(m, 1))

            @pl.when(p >= PRE_LATE)
            def _():
                each(early, m_all, lambda m: ring_arrived(m, 0))

            for c in late_copies():
                c.start()
            each(0, m_all, sent)

        @pl.when(j > 1)
        def _():
            for c in part_copies(j):
                c.wait()

        def put(v1, v2):
            for c in range(SLABS):
                for e in range(nd):
                    zs[m_all - 2 + j % 2, c * nd + e] = _cut(v2[c * LANES : (c + 1) * LANES], e)
                    full[j % 2, c * nd + e] = _cut(v1[e * LANES : (e + 1) * LANES], c)

        def block(ready):
            _dw_block(
                512, group(hw), group(gw), groups, rows, nd,
                lambda: _wide([w1v[j * SLABS + c] for c in range(SLABS)]),
                lambda: _wide([w2t[j * SLABS + c] for c in range(SLABS)]),
                ht, ab, zb, put, ready,
            )

        @pl.when(j < formed)
        def _():
            b = j % 2
            for c in pre_loads(j):
                c.wait()

            @pl.when(j + 1 < jnp.minimum(formed, units))
            def _():
                for c in pre_loads(j + 1):
                    c.start()

            block((
                lambda c: w2v[b * SLABS + c, 0:tokens, :],
                lambda k, c: zs[b, c * groups + k],
            ))

        @pl.when(j >= formed)
        def _():
            block(None)

        for c in part_copies(j):
            c.start()

    kept = (
        pltpu.make_async_copy(w1v, w1_out, keep_sem.at[0]), pltpu.make_async_copy(w2t, w2_out, keep_sem.at[1])
    )
    with jax.named_scope("loads"):
        for c in loads[:nf]:
            c.wait()

    first = jnp.where(p == last, 1, m_all)
    rest = m_all - first
    turn = jnp.where(p < n_stage // 2, first, 0)

    def step(k, carry):
        j = k - first
        swap = j < 2 * rest
        is_u = k >= 2 * m_all
        is_f = (j < 0) | (swap & (j % 2 == 1))
        is_b = jnp.logical_not(is_f | is_u)
        m_f = jnp.where(j < 0, k, jnp.minimum(first + j // 2, m_all - 1))
        m_b = jnp.maximum(jnp.minimum(jnp.where(swap, j // 2, j - rest), m_all - 1), 0)
        u = jnp.maximum(k - 2 * m_all, 0)

        @pl.when(k == turn)
        def _():
            with jax.named_scope("transp"):
                @pl.when(p >= n_stage // 2)
                def _():
                    for c in loads[nf:]:
                        c.wait()

                transpose_weights()
                for c in kept:
                    c.start()

        @pl.when((k == first) & (p < n_stage - 2))
        def _():
            with jax.named_scope("slopes"):
                slopes()
            with jax.named_scope("hring"):
                each(0, jnp.where(p < mid, m_all, early), lambda m: ring_forward(0, m, hw))

        @pl.when((k == first) & (p < n_stage // 2))
        def _():
            with jax.named_scope("pre"):
                each(0, early, lambda m: ring_arrived(m, 0))

                @pl.when(p < PRE_LATE)
                def _():
                    each(early, m_all, lambda m: ring_arrived(m, 0))

                _transposed_rows(group(hw), groups, rows, nd, ht)
                each(0, formed, pre_unit)
                for c in (*pre_stores(0), *pre_stores(1)):
                    c.wait()

        early_f, odd = is_f & (p < n_stage - 2), p % 2 == 1
        for when, sloped, split in (
            (early_f & jnp.logical_not(odd), False, False),
            (early_f & odd, False, True),
            (is_f & (p >= n_stage - 2), True, False),
        ):
            @pl.when(when)
            def _():
                with jax.named_scope("fwd"):
                    forward(m_f, sloped, split)

        leaves = (p > 0) & jnp.logical_not(odd)
        for when, split in ((is_b & leaves, True), (is_b & jnp.logical_not(leaves), False)):
            @pl.when(when)
            def _():
                with jax.named_scope("bwd"):
                    backward(m_b, split)

        @pl.when(is_u)
        def _():
            with jax.named_scope("unit"):
                unit(u)

        return carry

    lax.fori_loop(0, 2 * m_all + units, step, 0)

    with jax.named_scope("finish"):
        for c in (*kept, *part_copies(units - 2), *part_copies(units - 1), *late_copies()):
            c.wait()
    with jax.named_scope("outwait"):
        pltpu.make_async_copy(y.at[0], y.at[0], out_recv.at[0]).wait()
        pltpu.make_async_copy(dx.at[0], dx.at[0], out_recv.at[1]).wait()


def _chain(n_stage, n_inner, x, g, w1, w2):
    mb, rows, d = x.shape
    f = w1.shape[-1]
    rows = rows * MERGE
    m_all = mb * n_stage // MERGE
    early = EARLY
    nd, nf = d // LANES, f // LANES
    blk = SLABS * LANES
    groups = n_inner * early
    tokens = groups * rows
    tiles = SLABS * max(nd, groups)
    hbm = pl.BlockSpec(memory_space=pltpu.HBM)
    whole = (n_inner, m_all, nd, rows, LANES)
    late = jax.ShapeDtypeStruct((n_inner, m_all - early, nd, rows, LANES), BF16)
    dma = pltpu.SemaphoreType.DMA
    vmem = pltpu.VMEM
    return pl.pallas_call(
        functools.partial(_chain_kernel, n_stage, n_inner),
        out_shape=[
            jax.ShapeDtypeStruct(x.shape, BF16), jax.ShapeDtypeStruct(x.shape, BF16), late, late,
            jax.ShapeDtypeStruct((nf, d, LANES), BF16), jax.ShapeDtypeStruct((nf, d, LANES), BF16),
            jax.ShapeDtypeStruct((f // blk, SLABS * nd, LANES, LANES), F32),
            jax.ShapeDtypeStruct((f // blk, SLABS * nd, LANES, LANES), F32),
            jax.ShapeDtypeStruct((2 * f // blk, SLABS, tokens, LANES), BF16),
            jax.ShapeDtypeStruct((2 * f // blk, SLABS * groups, rows, LANES), F32),
        ],
        in_specs=[hbm] * 4,
        out_specs=[hbm] * 10,
        scratch_shapes=[
            vmem((nf, d, LANES), BF16), vmem((nd, f, LANES), BF16),
            vmem((nd, f, LANES), BF16), vmem((nf, d, LANES), BF16),
            vmem(whole, BF16), vmem(whole, BF16),
            vmem((m_all, nd, rows, LANES), BF16), vmem((m_all, nd, rows, LANES), BF16),
            vmem((m_all, nf, rows, LANES), F32), vmem((nf, rows, LANES), BF16),
            vmem((tokens // LANES, d, LANES), BF16),
            vmem((2, SLABS, tokens, LANES), BF16), vmem((2, tiles, LANES, LANES), F32),
            vmem((2, nd, rows // MERGE, LANES), BF16),
            dma((2,)), dma((2,)), dma((m_all,)), dma((m_all,)), dma((m_all,)), dma((m_all,)), dma((2,)),
            dma((2, m_all, 4)), dma((2, m_all, 4)), dma((2, 2)), dma((2, n_inner)), dma((2, 2)), dma((2,)), dma((2,)),
        ],
        compiler_params=pltpu.CompilerParams(
            collective_id=0, has_side_effects=True, vmem_limit_bytes=VMEM_LIMIT
        ),
        name="chain",
    )(x, g, w1, w2)


def _late_kernel(
    h, g, y_in, dx_in, w1, w2t, p1, p2, ap, sp, d1, d2, y, dx,
    hv, gv, w1v, w2v, p1v, p2v, av, sv, d1v, d2v, ht, ab, zb, yv, first_sem, load_sem, store_sem, pass_sem,
):
    groups, nd, rows, _ = h.shape
    units = w1.shape[0] // SLABS
    d, blk = d1v.shape[1:]

    def pre(j):
        return (lax.axis_index("stage") < PRE_LATE) & (j % 2 == 1)

    def weights(j):
        b, some = j % DEEP, pl.ds(j * SLABS, SLABS)
        return (pltpu.make_async_copy(w2t.at[some], w2v.at[b], load_sem.at[0, b]),)

    def own(j):
        b, some = j % DEEP, pl.ds(j * SLABS, SLABS)
        return (pltpu.make_async_copy(w1.at[some], w1v.at[b], load_sem.at[1, b]),)

    def ready(j):
        b = j % DEEP
        return (
            pltpu.make_async_copy(ap.at[units + j], av.at[b], load_sem.at[1, b]),
            pltpu.make_async_copy(sp.at[units + j], sv.at[b], load_sem.at[2, b]),
        )

    def parts(j):
        b = j % DEEP
        return (
            pltpu.make_async_copy(p1.at[j], p1v.at[b], load_sem.at[3, b]),
            pltpu.make_async_copy(p2.at[j], p2v.at[b], load_sem.at[4, b]),
        )

    def stores(j):
        b, some = j % 2, pl.ds(pl.multiple_of(j * blk, blk), blk)
        return (
            pltpu.make_async_copy(d1v.at[b], d1.at[:, some], store_sem.at[0, b]),
            pltpu.make_async_copy(d2v.at[b], d2.at[some, :], store_sem.at[1, b]),
        )

    def do(copies, how):
        for c in copies:
            getattr(c, how)()

    def inputs(j, how):
        @pl.when(pre(j))
        def _():
            do(ready(j), how)

        @pl.when(jnp.logical_not(pre(j)))
        def _():
            do(own(j), how)

        do(weights(j), how)

    firsts = (pltpu.make_async_copy(h, hv, first_sem.at[0]), pltpu.make_async_copy(g, gv, first_sem.at[1]))
    firsts[0].start()
    inputs(0, "start")
    firsts[1].start()
    do(parts(0), "start")
    into = [pltpu.make_async_copy(a, yv.at[n], pass_sem.at[n]) for n, a in enumerate((y_in, dx_in))]
    out_of = [pltpu.make_async_copy(yv.at[n], a, pass_sem.at[n]) for n, a in enumerate((y, dx))]
    do(into, "start")
    firsts[0].wait()
    _transposed_rows(lambda k, c: hv[k, c], groups, rows, nd, ht)
    do(into, "wait")
    do(out_of, "start")

    def unit(j, carry):
        b, n = j % 2, j % DEEP
        inputs(j, "wait")
        do(parts(j), "wait")

        @pl.when(j == 0)
        def _():
            firsts[1].wait()
            for e in range(1, DEEP - 1):
                inputs(e, "start")
                do(parts(e), "start")

        @pl.when(j + DEEP - 1 < units)
        def _():
            inputs(j + DEEP - 1, "start")
            do(parts(j + DEEP - 1), "start")

        @pl.when(j > 1)
        def _():
            do(stores(j), "wait")

        def put(v1, v2):
            for c in range(SLABS):
                for e in range(nd):
                    r, s = slice(e * LANES, (e + 1) * LANES), slice(c * LANES, (c + 1) * LANES)
                    d2v[b, s, r] = p2v[n, c * nd + e] + v2[s, r]
                    d1v[b, r, s] = p1v[n, c * nd + e] + v1[r, s]

        def block(ready):
            _dw_block(
                512, lambda k, c: hv[k, c], lambda k, c: gv[k, c], groups, rows, nd,
                lambda: _wide([w1v[n, c] for c in range(SLABS)]), lambda: _wide([w2v[n, c] for c in range(SLABS)]),
                ht, ab, zb, put, ready,
            )

        @pl.when(pre(j))
        def _():
            block((lambda c: av[n, c], lambda k, c: sv[n, c * groups + k]))

        @pl.when(jnp.logical_not(pre(j)))
        def _():
            block(None)

        do(stores(j), "start")
        return carry

    lax.fori_loop(0, units, unit, 0)
    do(stores(units - 2), "wait")
    do(stores(units - 1), "wait")
    do(out_of, "wait")


def _late(h, g, y, dx, w1, w2t, p1, p2, ap, sp):
    groups, nd, rows, _ = h.shape
    nf, d, _ = w1.shape
    f, blk, t = nf * LANES, SLABS * LANES, groups * rows
    hbm = pl.BlockSpec(memory_space=pltpu.HBM)
    vmem, dma = pltpu.VMEM, pltpu.SemaphoreType.DMA
    return pl.pallas_call(
        _late_kernel,
        in_specs=[hbm] * 10,
        out_specs=[hbm] * 4,
        out_shape=[
            jax.ShapeDtypeStruct((d, f), F32), jax.ShapeDtypeStruct((f, d), F32),
            jax.ShapeDtypeStruct(y.shape, BF16), jax.ShapeDtypeStruct(dx.shape, BF16),
        ],
        scratch_shapes=[
            vmem(h.shape, BF16), vmem(g.shape, BF16),
            vmem((DEEP, SLABS, d, LANES), BF16), vmem((DEEP, SLABS, d, LANES), BF16),
            vmem((DEEP, *p1.shape[1:]), F32), vmem((DEEP, *p2.shape[1:]), F32),
            vmem((DEEP, *ap.shape[1:]), BF16), vmem((DEEP, *sp.shape[1:]), F32),
            vmem((2, d, blk), F32), vmem((2, blk, d), F32),
            vmem((t // LANES, d, LANES), BF16), vmem((SLABS, t, LANES), BF16), vmem((SLABS, t, LANES), BF16),
            vmem((2, *y.shape), BF16),
            dma((2,)), dma((5, DEEP)), dma((2, 2)), dma((2,)),
        ],
        compiler_params=pltpu.CompilerParams(vmem_limit_bytes=VMEM_LIMIT),
        cost_estimate=pl.CostEstimate(flops=8 * t * d * f, bytes_accessed=20 * d * f, transcendentals=t * f),
        name="late",
    )(h, g, y, dx, w1, w2t, p1, p2, ap, sp)


def solution(mesh):
    n_stage, n_inner = mesh.shape["stage"], mesh.shape["inner"]

    def body(x, g, w1, w2):
        y, dx, h, gg, w1s, w2s, *parts = _chain(n_stage, n_inner, x, g, w1, w2)
        flat = (-1, *h.shape[2:])
        d1, d2, y, dx = _late(h.reshape(flat), gg.reshape(flat), y, dx, w1s, w2s, *parts)
        return y, dx, d1.reshape(w1.shape), d2.reshape(w2.shape)

    tok = P(("data", "stage"), "inner", None)
    wsp = P(None, "stage", None, None)
    dsp = P("data", "stage", None, None)
    return jax.shard_map(body, mesh=mesh, in_specs=(tok, tok, wsp, wsp), out_specs=(tok, tok, dsp, dsp), check_vma=False)
```

profile of v0, /device:TPU:96, one launch (start us, length us, event | category | flops | bytes accessed | tf_op | source)
XLA Modules:
  0.0 179.7 jit_solution(12241118594910064174)
XLA Ops:
  0.6 139.0 %chain.1 = (bf16[1,64,1024]{2,1,0:T(8,128)(2,1)}, bf16[1,64,1024]{2,1,0:T(8,128)(2,1)}, bf16[4,2,8,128,128]{4,3,2,1,0:T(8,128)(2,1)}, bf16[4,2,8,128,128]{4,3,2,...) custom-call(bf16[1,64,1024]{2,1,0:T(8,128)(2,1)} %x.1, ...), custom_call_target="tpu_custom_call" | custom-call | tf_op jit(solution)/shard_map/chain/pallas_call | solution.py:583
  139.6 39.9 %late.1 = (f32[1024,4096]{1,0:T(8,128)}, f32[4096,1024]{1,0:T(8,128)}, bf16[1,64,1024]{2,1,0:T(8,128)(2,1)}, bf16[1,64,1024]{2,1,0:T(8,128)(2,1)}) custom-call(bf16[8,8,128,128]{3,2,1,0:T(8,128)(2,1)} %bitcast.4, bf16[8,8,128,128]{3,2,1,0:T(8,128)(2,1)} %bitcast.5, bf16[1,64,1024]{2,1,0:T(8,128)(2,1)} %get-tuple-element.20.y_in, ...), custom_call_target="tpu_custom_call" | custom-call | flops 34359738368 | bytes 83886080 | tf_op jit(solution)/shard_map/late/pallas_call | solution.py:740
where the time goes:
time: 180 us
  Pallas kernels  179 us (99%)
    pallas_call x1, Pallas kernels, _chain(): pl.pallas_call(functools.partial(_chain_kernel, n_stage, n_inner), out_sh...  139 us
    pallas_call x1, Pallas kernels, _late(): pl.pallas_call(_late_kernel, in_specs=[hbm] * 10, out_specs=[hbm] * 4, ou...  39.9 us

commit v1 on v0

--- a/solution.py
+++ b/solution.py
@@ -162,14 +162,21 @@
         to_inner(a, a, ring_send.at[q, m, 0], ring_recv.at[q, m, 0], right).start()
         to_inner(a, a, ring_send.at[q, m, 1], ring_recv.at[q, m, 1], left).start()
 
-    def ring_forward(q, m, whole):
-        a, b = whole.at[left, m], whole.at[right, m]
+    def forward_right(q, m, whole):
+        a = whole.at[left, m]
         to_inner(a, a, ring_send.at[q, m, 0], ring_recv.at[q, m, 0], right).wait_recv()
         a = whole.at[left, m, pl.ds(0, half)]
         to_inner(a, a, ring_send.at[q, m, 2], ring_recv.at[q, m, 2], right).start()
+
+    def forward_left(q, m, whole):
+        b = whole.at[right, m]
         to_inner(b, b, ring_send.at[q, m, 1], ring_recv.at[q, m, 1], left).wait_recv()
         b = whole.at[right, m, pl.ds(half, half)]
         to_inner(b, b, ring_send.at[q, m, 3], ring_recv.at[q, m, 3], left).start()
+
+    def ring_forward(q, m, whole):
+        forward_right(q, m, whole)
+        forward_left(q, m, whole)
 
     def ring_far(q, m, whole):
         far = lax.rem(i + 2, n_inner)
@@ -253,6 +260,10 @@
         def _():
             ring_forward(1, early - 1, gw)
 
+        @pl.when((p < mid) & (m == 1))
+        def _():
+            forward_right(1, 0, gw)
+
         with jax.named_scope("wait_g"):
             pltpu.make_async_copy(gw.at[i, m], gw.at[i, m], g_recv.at[m]).wait()
 
@@ -272,9 +283,13 @@
         def _():
             ring_forward(0, 0, hw)
 
+        @pl.when((p < mid) & (m > 1) & (m <= early))
+        def _():
+            forward_right(1, jnp.maximum(m - 1, 0), gw)
+
         @pl.when((p < mid) & (m > 0) & (m <= early))
         def _():
-            ring_forward(1, jnp.maximum(m - 1, 0), gw)
+            forward_left(1, jnp.maximum(m - 1, 0), gw)
 
         @pl.when((p >= mid) & (p < n_stage - 2) & (m == early))
         def _():
@@ -341,7 +356,8 @@
             c.start()
 
     formed = jnp.where(
-        p < PRE_LATE, 2 * units, jnp.where(p < mid - 1, units, jnp.where(p == mid - 1, units // 2, 0))
+        p < PRE_LATE, 2 * units,
+        jnp.where(p < mid - 1, units, jnp.where(p == mid - 1, units * 3 // 4, jnp.where(p == mid, units // 2, 0))),
     )
 
     def part_copies(j):
@@ -399,20 +415,20 @@
                 each(1, early, lambda e: (ring_forward(0, e, hw), ring_forward(1, e, gw)))
 
 
-            @pl.when(p < n_stage // 2)
+            @pl.when(formed > 0)
             def _():
                 for c in pre_loads(0):
                     c.start()
 
             each(0, early, lambda m: ring_arrived(m, 1))
 
-            @pl.when(p >= n_stage // 2)
+            @pl.when(formed == 0)
             def _():
                 each(0, early, lambda m: ring_arrived(m, 0))
 
             each(early, m_all, firsts)
 
-            @pl.when(p >= mid)
+            @pl.when(formed == 0)
             def _():
                 _transposed_rows(group(hw), groups, rows, nd, ht)
 
@@ -515,7 +531,7 @@
             with jax.named_scope("hring"):
                 each(0, jnp.where(p < mid, m_all, early), lambda m: ring_forward(0, m, hw))
 
-        @pl.when((k == first) & (p < n_stage // 2))
+        @pl.when((k == first) & (formed > 0))
         def _():
             with jax.named_scope("pre"):
                 each(0, early, lambda m: ring_arrived(m, 0))

time: 180 us -> 181 us (level)
  no operation moved by 1% of the time
where the time goes in v1:
time: 181 us
  Pallas kernels  180 us (99%)
    pallas_call x1, Pallas kernels, _chain(): pl.pallas_call(functools.partial(_chain_kernel, n_stage, n_inner), out_sh...  140 us
    pallas_call x1, Pallas kernels, _late(): pl.pallas_call(_late_kernel, in_specs=[hbm] * 10, out_specs=[hbm] * 4, ou...  39.9 us

profile of v1, /device:TPU:96, one launch (start us, length us, event | category | flops | bytes accessed | tf_op | source)
XLA Modules:
  0.0 181.2 jit_solution(16756181578151815255)
XLA Ops:
  0.6 140.4 %chain.1 = (bf16[1,64,1024]{2,1,0:T(8,128)(2,1)}, bf16[1,64,1024]{2,1,0:T(8,128)(2,1)}, bf16[4,2,8,128,128]{4,3,2,1,0:T(8,128)(2,1)}, bf16[4,2,8,128,128]{4,3,2,...) custom-call(bf16[1,64,1024]{2,1,0:T(8,128)(2,1)} %x.1, ...), custom_call_target="tpu_custom_call" | custom-call | tf_op jit(solution)/shard_map/chain/pallas_call | solution.py:599
  141.1 39.9 %late.1 = (f32[1024,4096]{1,0:T(8,128)}, f32[4096,1024]{1,0:T(8,128)}, bf16[1,64,1024]{2,1,0:T(8,128)(2,1)}, bf16[1,64,1024]{2,1,0:T(8,128)(2,1)}) custom-call(bf16[8,8,128,128]{3,2,1,0:T(8,128)(2,1)} %bitcast.4, bf16[8,8,128,128]{3,2,1,0:T(8,128)(2,1)} %bitcast.5, bf16[1,64,1024]{2,1,0:T(8,128)(2,1)} %get-tuple-element.20.y_in, ...), custom_call_target="tpu_custom_call" | custom-call | flops 34359738368 | bytes 83886080 | tf_op jit(solution)/shard_map/late/pallas_call | solution.py:756

commit v2 on v1

--- a/solution.py
+++ b/solution.py
@@ -222,34 +222,67 @@
                     for c in range(nd):
                         pltpu.make_async_copy(src.at[m, c, piece(e)], flat(out, c), out_sem).start()
 
-    def project(m, split, res, w, src, *rest):
-        whole = _wide([act[c] for c in range(nf)])
+    def step_of(m, split, x_in, wa, activate, second, wb, src, *rest):
+        blocks, k_half = nf // SLABS, nf // 2
+        early_acts = blocks // 2 if second is None else blocks - 1
+        zs_in = []
+
+        def act_of(b):
+            a = activate(b * SLABS, zs_in[b])
+            for c in range(SLABS):
+                act[b * SLABS + c] = _cut(a, c)
+
+        def part_dot(lo, count, k):
+            a = _wide([act[k + c] for c in range(k_half)])
+            return _dot(a, _wide([wb[lo + c, k * LANES : (k + k_half) * LANES, :] for c in range(count)]))
+
+        for b in range(blocks):
+            zs_in.append(_dot(x_in, _wide([wa[b * SLABS + c] for c in range(SLABS)])))
+            if 0 < b <= early_acts:
+                act_of(b - 1)
+        if second is not None:
+            act_of(blocks - 1)
+            second()
         count = half if split else nd
         for lo in range(0, nd, count):
-            u = _dot(whole, _wide([w[lo + c] for c in range(count)]))
-            out = (res[:, lo * LANES : (lo + count) * LANES].astype(F32) + u).astype(BF16)
+            u = part_dot(lo, count, 0)
+            if lo == 0 and second is None:
+                for b in range(early_acts, blocks):
+                    act_of(b)
+            u = u + part_dot(lo, count, k_half)
+            out = (x_in[:, lo * LANES : (lo + count) * LANES].astype(F32) + u).astype(BF16)
             for c in range(count):
                 src[m, lo + c] = _cut(out, c)
             pass_on(m, lo, lo + count, src, *rest)
 
+    def second_weights():
+        for c in loads[nf:]:
+            c.wait()
+
     def forward(m, sloped, split):
+        @pl.when((m == 0) & (p > 0) & (p < mid))
+        def _():
+            second_weights()
+
         with jax.named_scope("wait_h"):
             pltpu.make_async_copy(hw.at[i, m], hw.at[i, m], h_recv.at[m]).wait()
         h = _wide([hw[i, m, c] for c in range(nd)])
-        for b in range(0, nf, SLABS):
-            z = _dot(h, _wide([w1v[b + c] for c in range(SLABS)]))
+
+        def activate(b, z):
             a, slope = _gelu_and_slope(z)
-            a, kept = a.astype(BF16), slope if sloped else z
             for c in range(SLABS):
-                zs[m, b + c] = _cut(kept, c)
-                act[b + c] = _cut(a, c)
-
-        @pl.when((m == 0) & (p < n_stage // 2))
-        def _():
-            for c in loads[nf:]:
-                c.wait()
-
-        project(m, split, h, w2v, ho, hw, h_send, h_recv, last, jnp.minimum(p + 1, last), y, out_recv.at[0])
+                zs[m, b + c] = _cut(slope if sloped else z, c)
+            return a.astype(BF16)
+
+        def second():
+            @pl.when((m == 0) & (p == 0))
+            def _():
+                second_weights()
+
+        step_of(
+            m, split, h, w1v, activate, None if sloped or split else second, w2v,
+            ho, hw, h_send, h_recv, last, jnp.minimum(p + 1, last), y, out_recv.at[0],
+        )
 
         @pl.when((p < mid) | (m < early))
         def _():
@@ -260,10 +293,6 @@
         def _():
             ring_forward(1, early - 1, gw)
 
-        @pl.when((p < mid) & (m == 1))
-        def _():
-            forward_right(1, 0, gw)
-
         with jax.named_scope("wait_g"):
             pltpu.make_async_copy(gw.at[i, m], gw.at[i, m], g_recv.at[m]).wait()
 
@@ -272,24 +301,18 @@
             ring_first(1, m, gw)
 
         dh = _wide([gw[i, m, c] for c in range(nd)])
-        for b in range(0, nf, SLABS):
-            da = _dot(dh, _wide([w2t[b + c] for c in range(SLABS)]))
-            dz = (da * _wide([zs[m, b + c] for c in range(SLABS)])).astype(BF16)
-            for c in range(SLABS):
-                act[b + c] = _cut(dz, c)
-        project(m, split, dh, w1t, go, gw, g_send, g_recv, 0, jnp.maximum(p - 1, 0), dx, out_recv.at[1])
+        step_of(
+            m, split, dh, w2t, lambda b, da: (da * _wide([zs[m, b + c] for c in range(SLABS)])).astype(BF16), None,
+            w1t, go, gw, g_send, g_recv, 0, jnp.maximum(p - 1, 0), dx, out_recv.at[1],
+        )
 
         @pl.when((p >= n_stage - 2) & (m == early))
         def _():
             ring_forward(0, 0, hw)
 
-        @pl.when((p < mid) & (m > 1) & (m <= early))
-        def _():
-            forward_right(1, jnp.maximum(m - 1, 0), gw)
-
         @pl.when((p < mid) & (m > 0) & (m <= early))
         def _():
-            forward_left(1, jnp.maximum(m - 1, 0), gw)
+            ring_forward(1, jnp.maximum(m - 1, 0), gw)
 
         @pl.when((p >= mid) & (p < n_stage - 2) & (m == early))
         def _():
@@ -357,7 +380,7 @@
 
     formed = jnp.where(
         p < PRE_LATE, 2 * units,
-        jnp.where(p < mid - 1, units, jnp.where(p == mid - 1, units * 3 // 4, jnp.where(p == mid, units // 2, 0))),
+        jnp.where(p < mid - 1, units, jnp.where(p == mid - 1, units * 3 // 4, 0)),
     )
 
     def part_copies(j):

time: 181 us -> 179 us (0.989)
  Pallas kernels: 180 us -> 178 us
    pallas_call x1, Pallas kernels: 140 us -> 138 us  [_chain(): pl.pallas_call(functools.partial(_chain_kernel, n_stage, n_inner), out_sh...]
where the time goes in v2:
time: 179 us
  Pallas kernels  178 us (99%)
    pallas_call x1, Pallas kernels, _chain(): pl.pallas_call(functools.partial(_chain_kernel, n_stage, n_inner), out_sh...  138 us
    pallas_call x1, Pallas kernels, _late(): pl.pallas_call(_late_kernel, in_specs=[hbm] * 10, out_specs=[hbm] * 4, ou...  39.9 us

profile of v2, /device:TPU:96, one launch (start us, length us, event | category | flops | bytes accessed | tf_op | source)
XLA Modules:
  0.0 178.8 jit_solution(7489555945489095299)
XLA Ops:
  0.6 138.0 %chain.1 = (bf16[1,64,1024]{2,1,0:T(8,128)(2,1)}, bf16[1,64,1024]{2,1,0:T(8,128)(2,1)}, bf16[4,2,8,128,128]{4,3,2,1,0:T(8,128)(2,1)}, bf16[4,2,8,128,128]{4,3,2,...) custom-call(bf16[1,64,1024]{2,1,0:T(8,128)(2,1)} %x.1, ...), custom_call_target="tpu_custom_call" | custom-call | tf_op jit(solution)/shard_map/chain/pallas_call | solution.py:622
  138.7 39.9 %late.1 = (f32[1024,4096]{1,0:T(8,128)}, f32[4096,1024]{1,0:T(8,128)}, bf16[1,64,1024]{2,1,0:T(8,128)(2,1)}, bf16[1,64,1024]{2,1,0:T(8,128)(2,1)}) custom-call(bf16[8,8,128,128]{3,2,1,0:T(8,128)(2,1)} %bitcast.4, bf16[8,8,128,128]{3,2,1,0:T(8,128)(2,1)} %bitcast.5, bf16[1,64,1024]{2,1,0:T(8,128)(2,1)} %get-tuple-element.20.y_in, ...), custom_call_target="tpu_custom_call" | custom-call | flops 34359738368 | bytes 83886080 | tf_op jit(solution)/shard_map/late/pallas_call | solution.py:779

commit v3 on v2

--- a/solution.py
+++ b/solution.py
@@ -157,46 +157,48 @@
     own(own_v.at[0], hw, h_recv, xsem.at[0], 0)
     own(own_v.at[1], gw, g_recv, xsem.at[1], last)
 
+    low, high = pl.ds(0, half), pl.ds(half, half)
+
+    def ring_own(q, m, whole):
+        kinds = ((0, low, right), (1, high, left), (4, high, right), (5, low, left))
+        return [
+            to_inner(
+                whole.at[i, m, some], whole.at[i, m, some], ring_send.at[q, m, k], ring_recv.at[q, m, k], inner
+            )
+            for k, some, inner in kinds
+        ]
+
     def ring_first(q, m, whole):
-        a = whole.at[i, m]
-        to_inner(a, a, ring_send.at[q, m, 0], ring_recv.at[q, m, 0], right).start()
-        to_inner(a, a, ring_send.at[q, m, 1], ring_recv.at[q, m, 1], left).start()
-
-    def forward_right(q, m, whole):
-        a = whole.at[left, m]
-        to_inner(a, a, ring_send.at[q, m, 0], ring_recv.at[q, m, 0], right).wait_recv()
-        a = whole.at[left, m, pl.ds(0, half)]
-        to_inner(a, a, ring_send.at[q, m, 2], ring_recv.at[q, m, 2], right).start()
-
-    def forward_left(q, m, whole):
-        b = whole.at[right, m]
-        to_inner(b, b, ring_send.at[q, m, 1], ring_recv.at[q, m, 1], left).wait_recv()
-        b = whole.at[right, m, pl.ds(half, half)]
-        to_inner(b, b, ring_send.at[q, m, 3], ring_recv.at[q, m, 3], left).start()
+        for c in ring_own(q, m, whole):
+            c.start()
+
+    def ring_relay(q, m, whole, k):
+        src, some, inner = (left, low, right) if k == 0 else (right, high, left)
+        a = whole.at[src, m, some]
+        return (
+            to_inner(a, a, ring_send.at[q, m, k], ring_recv.at[q, m, k], inner),
+            to_inner(a, a, ring_send.at[q, m, 2 + k], ring_recv.at[q, m, 2 + k], inner),
+        )
 
     def ring_forward(q, m, whole):
-        forward_right(q, m, whole)
-        forward_left(q, m, whole)
-
-    def ring_far(q, m, whole):
+        for k in (0, 1):
+            arrival, onward = ring_relay(q, m, whole, k)
+            arrival.wait_recv()
+            onward.start()
+
+    def ring_arrived(m, q):
+        whole = (hw, gw)[q]
         far = lax.rem(i + 2, n_inner)
-        a, b = whole.at[far, m, pl.ds(0, half)], whole.at[far, m, pl.ds(half, half)]
-        return (
-            to_inner(a, a, ring_send.at[q, m, 2], ring_recv.at[q, m, 2], right),
-            to_inner(b, b, ring_send.at[q, m, 3], ring_recv.at[q, m, 3], left),
-        )
-
-    def ring_arrived(m, q):
-        for c in ring_far(q, m, (hw, gw)[q]):
-            c.wait_recv()
+        for k, src, some in ((4, left, high), (5, right, low), (2, far, low), (3, far, high)):
+            a = whole.at[src, m, some]
+            to_inner(a, a, ring_send.at[q, m, k], ring_recv.at[q, m, k], right).wait_recv()
 
     def ring_sent(m):
         for q, whole in ((0, hw), (1, gw)):
-            for c in ring_far(q, m, whole):
+            for c in ring_own(q, m, whole):
                 c.wait_send()
-            a = whole.at[i, m]
-            to_inner(a, a, ring_send.at[q, m, 0], ring_recv.at[q, m, 0], right).wait_send()
-            to_inner(a, a, ring_send.at[q, m, 1], ring_recv.at[q, m, 1], left).wait_send()
+            for k in (0, 1):
+                ring_relay(q, m, whole, k)[1].wait_send()
 
     def pass_on(m, lo, hi, src, slots, send, recv, end, nxt, out, out_sem):
         @pl.when(p != end)
@@ -293,6 +295,10 @@
         def _():
             ring_forward(1, early - 1, gw)
 
+        @pl.when((p < mid) & (m == 1))
+        def _():
+            ring_forward(1, 0, gw)
+
         with jax.named_scope("wait_g"):
             pltpu.make_async_copy(gw.at[i, m], gw.at[i, m], g_recv.at[m]).wait()
 
@@ -310,7 +316,7 @@
         def _():
             ring_forward(0, 0, hw)
 
-        @pl.when((p < mid) & (m > 0) & (m <= early))
+        @pl.when((p < mid) & (m > 1) & (m <= early))
         def _():
             ring_forward(1, jnp.maximum(m - 1, 0), gw)
 
@@ -470,7 +476,6 @@
 
             for c in late_copies():
                 c.start()
-            each(0, m_all, sent)
 
         @pl.when(j > 1)
         def _():
@@ -596,6 +601,7 @@
     lax.fori_loop(0, 2 * m_all + units, step, 0)
 
     with jax.named_scope("finish"):
+        each(0, m_all, sent)
         for c in (*kept, *part_copies(units - 2), *part_copies(units - 1), *late_copies()):
             c.wait()
     with jax.named_scope("outwait"):
@@ -641,7 +647,7 @@
             vmem((2, SLABS, tokens, LANES), BF16), vmem((2, tiles, LANES, LANES), F32),
             vmem((2, nd, rows // MERGE, LANES), BF16),
             dma((2,)), dma((2,)), dma((m_all,)), dma((m_all,)), dma((m_all,)), dma((m_all,)), dma((2,)),
-            dma((2, m_all, 4)), dma((2, m_all, 4)), dma((2, 2)), dma((2, n_inner)), dma((2, 2)), dma((2,)), dma((2,)),
+            dma((2, m_all, 6)), dma((2, m_all, 6)), dma((2, 2)), dma((2, n_inner)), dma((2, 2)), dma((2,)), dma((2,)),
         ],
         compiler_params=pltpu.CompilerParams(
             collective_id=0, has_side_effects=True, vmem_limit_bytes=VMEM_LIMIT

time: 179 us -> 179 us (level)
  no operation moved by 1% of the time
where the time goes in v3:
time: 179 us
  Pallas kernels  178 us (99%)
    pallas_call x1, Pallas kernels, _chain(): pl.pallas_call(functools.partial(_chain_kernel, n_stage, n_inner), out_sh...  138 us
    pallas_call x1, Pallas kernels, _late(): pl.pallas_call(_late_kernel, in_specs=[hbm] * 10, out_specs=[hbm] * 4, ou...  39.9 us

profile of v3, /device:TPU:96, one launch (start us, length us, event | category | flops | bytes accessed | tf_op | source)
XLA Modules:
  0.0 178.9 jit_solution(8033114682181080101)
XLA Ops:
  0.6 138.1 %chain.1 = (bf16[1,64,1024]{2,1,0:T(8,128)(2,1)}, bf16[1,64,1024]{2,1,0:T(8,128)(2,1)}, bf16[4,2,8,128,128]{4,3,2,1,0:T(8,128)(2,1)}, bf16[4,2,8,128,128]{4,3,2,...) custom-call(bf16[1,64,1024]{2,1,0:T(8,128)(2,1)} %x.1, ...), custom_call_target="tpu_custom_call" | custom-call | tf_op jit(solution)/shard_map/chain/pallas_call | solution.py:628
  138.8 39.9 %late.1 = (f32[1024,4096]{1,0:T(8,128)}, f32[4096,1024]{1,0:T(8,128)}, bf16[1,64,1024]{2,1,0:T(8,128)(2,1)}, bf16[1,64,1024]{2,1,0:T(8,128)(2,1)}) custom-call(bf16[8,8,128,128]{3,2,1,0:T(8,128)(2,1)} %bitcast.4, bf16[8,8,128,128]{3,2,1,0:T(8,128)(2,1)} %bitcast.5, bf16[1,64,1024]{2,1,0:T(8,128)(2,1)} %get-tuple-element.20.y_in, ...), custom_call_target="tpu_custom_call" | custom-call | flops 34359738368 | bytes 83886080 | tf_op jit(solution)/shard_map/late/pallas_call | solution.py:785

commit v4 on v2

--- a/solution.py
+++ b/solution.py
@@ -659,7 +659,7 @@
     d, blk = d1v.shape[1:]
 
     def pre(j):
-        return (lax.axis_index("stage") < PRE_LATE) & (j % 2 == 1)
+        return (lax.axis_index("stage") < PRE_LATE) & ((j % 2 == 1) | (j == units - 2))
 
     def weights(j):
         b, some = j % DEEP, pl.ds(j * SLABS, SLABS)

time: 179 us -> 177 us (0.989)
  no operation moved by 1% of the time
where the time goes in v4:
time: 177 us
  Pallas kernels  177 us (100%)
    pallas_call x1, Pallas kernels, _chain(): pl.pallas_call(functools.partial(_chain_kernel, n_stage, n_inner), out_sh...  138 us
    pallas_call x1, Pallas kernels, _late(): pl.pallas_call(_late_kernel, in_specs=[hbm] * 10, out_specs=[hbm] * 4, ou...  38.5 us

profile of v4, /device:TPU:96, one launch (start us, length us, event | category | flops | bytes accessed | tf_op | source)
XLA Modules:
  0.0 177.3 jit_solution(16692661555165926309)
XLA Ops:
  0.6 138.0 %chain.1 = (bf16[1,64,1024]{2,1,0:T(8,128)(2,1)}, bf16[1,64,1024]{2,1,0:T(8,128)(2,1)}, bf16[4,2,8,128,128]{4,3,2,1,0:T(8,128)(2,1)}, bf16[4,2,8,128,128]{4,3,2,...) custom-call(bf16[1,64,1024]{2,1,0:T(8,128)(2,1)} %x.1, ...), custom_call_target="tpu_custom_call" | custom-call | tf_op jit(solution)/shard_map/chain/pallas_call | solution.py:622
  138.7 38.5 %late.1 = (f32[1024,4096]{1,0:T(8,128)}, f32[4096,1024]{1,0:T(8,128)}, bf16[1,64,1024]{2,1,0:T(8,128)(2,1)}, bf16[1,64,1024]{2,1,0:T(8,128)(2,1)}) custom-call(bf16[8,8,128,128]{3,2,1,0:T(8,128)(2,1)} %bitcast.4, bf16[8,8,128,128]{3,2,1,0:T(8,128)(2,1)} %bitcast.5, bf16[1,64,1024]{2,1,0:T(8,128)(2,1)} %get-tuple-element.20.y_in, ...), custom_call_target="tpu_custom_call" | custom-call | flops 34359738368 | bytes 83886080 | tf_op jit(solution)/shard_map/late/pallas_call | solution.py:779
